TPU v7x, 32 devices: a whole 2x2x4 slice. The times are simulated.
32 devices in a mesh: rep: 4 (over x, y), dp: 8 (over z, core).
Axes of the slice: x: 2, y: 2, z: 4, core: 2. Of those that a mesh axis runs over, the one named last changes fastest.
Arguments:
- x: bfloat16 [32, 2048, 896], P(('rep', 'dp')), parts along dimension 0
- dy: bfloat16 [32, 2048, 896], P(('rep', 'dp')), parts along dimension 0
- w_gate: bfloat16 [2, 896, 2304], replicated
- w_up: bfloat16 [2, 896, 2304], replicated
- w_down: bfloat16 [2, 2304, 896], replicated
- m_w_gate: float32 [2, 896, 2304], replicated
- m_w_up: float32 [2, 896, 2304], replicated
- m_w_down: float32 [2, 2304, 896], replicated
- v_w_gate: float32 [2, 896, 2304], replicated
- v_w_up: float32 [2, 896, 2304], replicated
- v_w_down: float32 [2, 2304, 896], replicated
Outputs:
- output 1: bfloat16 [8, 896, 2304], P('rep'), parts along dimension 0
- output 2: bfloat16 [8, 896, 2304], P('rep'), parts along dimension 0
- output 3: bfloat16 [8, 2304, 896], P('rep'), parts along dimension 0
- output 4: float32 [8, 896, 2304], P('rep'), parts along dimension 0
- output 5: float32 [8, 896, 2304], P('rep'), parts along dimension 0
- output 6: float32 [8, 2304, 896], P('rep'), parts along dimension 0
- output 7: float32 [8, 896, 2304], P('rep'), parts along dimension 0
- output 8: float32 [8, 896, 2304], P('rep'), parts along dimension 0
- output 9: float32 [8, 2304, 896], P('rep'), parts along dimension 0
There are 4 independent parts. A program takes and returns all parts, laid end to end along the dimension named above; an argument that names none is the same for every part.
All inputs are finite; a program needn't handle non-finite values.
Results may differ from a plain program's by a relative error of at most 0.02.
Values are sent between devices in bfloat16 or wider.
A program may use at most 2.5 GiB of HBM per device.

v0:
```python
import jax
import jax.numpy as jnp
from jax import lax
from jax.sharding import PartitionSpec as P

NAMES = ("w_gate", "w_up", "w_down")


def matmul(a, w):
    return jnp.dot(a, w, preferred_element_type=jnp.float32).astype(jnp.bfloat16)


def normed(h):
    wide = h.astype(jnp.float32)
    scale = lax.rsqrt(jnp.mean(wide**2, -1, keepdims=True) + 1e-6)
    return (wide * scale).astype(jnp.bfloat16)


def layer(h, w):
    a = normed(h)
    gate = jnp.dot(a, w["w_gate"], preferred_element_type=jnp.float32)
    up = jnp.dot(a, w["w_up"], preferred_element_type=jnp.float32)
    return h + matmul((jax.nn.silu(gate) * up).astype(jnp.bfloat16), w["w_down"])


def adamw(w, m, v, g):
    m = 0.9 * m + 0.1 * g
    v = 0.95 * v + 0.05 * g * g
    step = m * lax.rsqrt(v + 1e-8) + 0.1 * w
    return (w - 0.02 * step).astype(jnp.bfloat16), m, v


def solution(mesh):
    def step(x, dy, *arrays):
        weights, m, v = (arrays[i : i + 3] for i in (0, 3, 6))
        layers = weights[0].shape[0]
        h, kept = x[0], []
        for number in range(layers):
            kept.append(h)
            h = layer(h, {name: w[number] for name, w in zip(NAMES, weights, strict=True)})
        by_h, summed = dy[0], [None] * layers
        for number in reversed(range(layers)):
            _, back = jax.vjp(lambda w, h: layer(h, w), {name: w[number] for name, w in zip(NAMES, weights, strict=True)}, kept[number])
            by_w, by_h = back(by_h)
            summed[number] = [lax.psum(by_w[name], "dp") for name in NAMES]
        gradients = [jnp.stack([summed[number][i] for number in range(layers)]).astype(jnp.float32) for i in range(3)]
        new = [adamw(w.astype(jnp.float32), m, v, g) for w, m, v, g in zip(weights, m, v, gradients, strict=True)]
        return tuple(one[which] for which in range(3) for one in new)

    return jax.shard_map(
        step,
        mesh=mesh,
        in_specs=(P(("rep", "dp"), None, None),) * 2 + (P(None, None, None),) * 9,
        out_specs=(P("rep", None, None),) * 9,
        check_vma=False,
    )
```

profile of v0, /device:TPU:0, one launch (start us, length us, event | category | flops | bytes accessed | tf_op | source)
XLA Modules:
  0.0 866.2 jit_solution(7421072194161459140)
XLA Ops:
  7.2 0.0 all-reduce.3.cloned.1.call-start
  7.2 6.1 copy.20
  13.3 2.8 fusion.30
  16.1 0.0 copy-start.8
  16.1 6.1 copy.21
  22.3 0.0 copy-start.2
  22.3 15.2 %convolution_convert_fusion.1 = bf16[2048,2304]{1,0:T(8,128)(2,1)} fusion(bf16[2,2304,896]{2,1,0:T(8,128)(2,1)} %param.15, bf16[1,2048,896]{2,1,0:T(8,128)(2,1)} %param.12), kind=kOutput, calls=%fused_computation.54 | convolution fusion | flops 8460435456 | bytes 17235968 | tf_op jit(solution)/shard_map/transpose(jvp())/dot_general | solution.py:10
  37.5 0.0 copy-done.2
  37.5 15.5 %fusion.64 = f32[2048,2304]{1,0:T(8,128)} fusion(bf16[2,896,2304]{2,1,0:T(8,128)(2,1)} %param.13, bf16[1,2048,896]{2,1,0:T(8,128)(2,1)S(1)} %copy-done.2, f32[2048]{0:T(1024)S(1)} %add_rsqrt_fusion), kind=kOutput, calls=%fused_computation.96 | convolution fusion | flops 8461221888 | bytes 26681344 | tf_op jit(solution)/shard_map/dot_general | solution.py:21
  53.0 0.0 copy-done.8
  53.0 21.6 %multiply_convert_fusion.1 = (bf16[2048,2304]{1,0:T(8,128)(2,1)}, f32[2048,2304]{1,0:T(8,128)}) fusion(f32[2048,2304]{1,0:T(8,128)} %fusion.64, bf16[2,896,2304]{2,1,0:T(8,128)(2,1)} %param.14, bf16[1,2048,896]{2,1,0:T(8,128)(2,1)} %param.11, f32[2048]{0:T(1024)S(1)} %add_rsqrt_fusion), kind=kOutput, calls=%fused_computation.29 | convolution fusion | flops 8489533440 | bytes 54992896 | tf_op jit(solution)/shard_map/dot_general | solution.py:22
  74.5 13.9 %fusion.34 = (f32[2048]{0:T(1024)S(1)}, bf16[2048,896]{0,1:T(8,128)(2,1)S(1)}) fusion(bf16[2048,2304]{1,0:T(8,128)(2,1)} %get-tuple-element.24, bf16[2,2304,896]{2,1,0:T(8,128)(2,1)} %param.15, bf16[1,2048,896]{1,2,0:T(8,128)(2,1)} %copy.20), kind=kOutput, calls=%fused_computation.67 | convolution fusion | flops 8464889856 | bytes 20914176 | tf_op jit(solution)/shard_map/dot_general | solution.py:10
  88.5 0.0 copy-start.3
  88.5 0.0 copy-start.6
  88.5 16.3 %fusion.51 = f32[2048,2304]{1,0:T(8,128)} fusion(bf16[2,896,2304]{2,1,0:T(8,128)(2,1)} %param.14, bf16[2048,896]{0,1:T(8,128)(2,1)S(1)} %get-tuple-element.27, f32[2048]{0:T(1024)S(1)} %fusion.92), kind=kOutput, calls=%fused_computation.83 | convolution fusion | flops 8461221888 | bytes 26681344 | tf_op jit(solution)/shard_map/jvp()/dot_general | solution.py:22
  104.9 0.0 copy-done.3
  104.9 0.0 copy-done.6
  104.9 26.3 %fusion.2 = (bf16[2048,2304]{1,0:T(8,128)(2,1)}, f32[2048,2304]{1,0:T(8,128)}) fusion(f32[2048,2304]{1,0:T(8,128)} %fusion.51, bf16[2048,2304]{1,0:T(8,128)(2,1)} %convolution_convert_fusion.1, bf16[2,896,2304]{2,1,0:T(8,128)(2,1)} %param.13, bf16[2048,896]{0,1:T(8,128)(2,1)S(1)} %get-tuple-element.27, f32[2048]{0:T(1024)S(1)} %fusion.92), kind=kOutput, calls=%fused_computation.20 | convolution fusion | flops 8517844992 | bytes 64430080 | tf_op jit(solution)/shard_map/jvp()/dot_general | solution.py:21
  131.2 17.2 %fusion.27 = bf16[2048,896]{0,1:T(8,128)(2,1)} fusion(bf16[2048,2304]{1,0:T(8,128)(2,1)} %convolution_convert_fusion.1, bf16[2,896,2304]{2,1,0:T(8,128)(2,1)} %param.14, f32[2048,2304]{1,0:T(8,128)} %get-tuple-element.29), kind=kOutput, calls=%fused_computation.48 | convolution fusion | flops 8484028416 | bytes 36110336 | tf_op jit(solution)/shard_map/transpose(jvp())/dot_general | solution.py:22
  148.3 18.0 %fusion.47 = bf16[1,896,2304]{2,1,0:T(8,128)(2,1)} fusion(bf16[2048,2304]{1,0:T(8,128)(2,1)} %convolution_convert_fusion.1, bf16[2048,896]{0,1:T(8,128)(2,1)} %copy-done.3, f32[2048]{0:T(1024)S(1)} %fusion.92, f32[2048,2304]{1,0:T(8,128)} %get-tuple-element.29), kind=kOutput, calls=%fused_computation.79 | convolution fusion | flops 8491597824 | bytes 36118528 | tf_op jit(solution)/shard_map/transpose(jvp())/dot_general | solution.py:22
  166.4 19.7 %fusion.49 = bf16[1,2304,896]{2,1,0:T(8,128)(2,1)} fusion(f32[2048,2304]{1,0:T(8,128)} %fusion.51, bf16[1,2048,896]{2,1,0:T(8,128)(2,1)} %param.12, f32[2048,2304]{1,0:T(8,128)} %get-tuple-element.29), kind=kOutput, calls=%fused_computation.81 | convolution fusion | flops 8486092800 | bytes 45547520 | tf_op jit(solution)/shard_map/transpose(jvp())/dot_general | solution.py:10
  186.0 0.0 copy-start.4
  186.0 0.0 slice-start
  186.0 14.6 %fusion.48 = bf16[1,896,2304]{2,1,0:T(8,128)(2,1)} fusion(bf16[2048,2304]{1,0:T(8,128)(2,1)} %get-tuple-element.28, bf16[2048,896]{0,1:T(8,128)(2,1)} %copy-done.3, f32[2048]{0:T(1024)S(1)} %fusion.92), kind=kOutput, calls=%fused_computation.80 | convolution fusion | flops 8461221888 | bytes 17244160 | tf_op jit(solution)/shard_map/transpose(jvp())/dot_general | solution.py:21
  200.6 0.0 copy-done.4
  200.6 0.0 copy-start.7
  200.6 0.0 copy-start.1
  200.6 0.0 slice-start.1
  200.6 13.8 %fusion.36 = (f32[2048]{0:T(1024)S(1)}, bf16[2048,896]{0,1:T(8,128)(2,1)S(1)}) fusion(bf16[2048,896]{0,1:T(8,128)(2,1)S(1)} %copy-done.4, bf16[2048,896]{0,1:T(8,128)(2,1)} %fusion.27, bf16[2048,2304]{1,0:T(8,128)(2,1)} %get-tuple-element.28, bf16[2,896,2304]{2,1,0:T(8,128)(2,1)} %param.13), kind=kOutput, calls=%fused_computation.69 | convolution fusion | flops 8464889856 | bytes 24584192 | tf_op jit(solution)/shard_map/transpose(jvp())/dot_general | solution.py:21
  214.4 0.0 copy-done.7
  214.4 0.0 copy-done.1
  214.5 4.6 fusion.70
  219.1 0.0 slice-done
  219.1 0.0 slice-done.1
  219.1 0.0 copy-start.5
  219.1 14.6 %convolution_convert_fusion = bf16[2048,2304]{1,0:T(8,128)(2,1)} fusion(bf16[2048,896]{0,1:T(8,128)(2,1)} %fusion.70, bf16[2,2304,896]{2,1,0:T(8,128)(2,1)S(1)} %bitcast.75), kind=kOutput, calls=%fused_computation.53 | convolution fusion | flops 8460435456 | bytes 17235968 | tf_op jit(solution)/shard_map/transpose(jvp())/dot_general | solution.py:10
  233.7 0.0 copy-done.5
  233.7 0.0 copy-start
  233.7 0.0 copy-start.9
  233.7 14.1 %fusion.50 = bf16[1,2304,896]{2,1,0:T(8,128)(2,1)} fusion(bf16[2048,2304]{1,0:T(8,128)(2,1)} %get-tuple-element.24, bf16[2048,896]{0,1:T(8,128)(2,1)S(1)} %copy-done.5), kind=kOutput, calls=%fused_computation.82 | convolution fusion | flops 8457781248 | bytes 17235968 | tf_op jit(solution)/shard_map/transpose(jvp())/dot_general | solution.py:10
  247.8 0.0 copy-done
  247.8 0.0 copy-done.9
  247.8 17.3 %fusion.43 = bf16[1,896,2304]{2,1,0:T(8,128)(2,1)} fusion(bf16[2048,2304]{1,0:T(8,128)(2,1)} %convolution_convert_fusion, bf16[1,2048,896]{1,2,0:T(8,128)(2,1)S(1)} %copy-done, f32[2048]{0:T(1024)S(1)} %copy-done.9, f32[2048,2304]{1,0:T(8,128)} %fusion.64), kind=kOutput, calls=%fused_computation.77 | convolution fusion | flops 8491597824 | bytes 36118528 | tf_op jit(solution)/shard_map/transpose(jvp())/dot_general | solution.py:22
  265.1 20.8 %fusion.44 = bf16[1,896,2304]{2,1,0:T(8,128)(2,1)} fusion(f32[2048,2304]{1,0:T(8,128)} %fusion.64, f32[2048,2304]{1,0:T(8,128)} %get-tuple-element.25, bf16[2048,2304]{1,0:T(8,128)(2,1)} %convolution_convert_fusion, bf16[1,2048,896]{1,2,0:T(8,128)(2,1)S(1)} %copy-done, f32[2048]{0:T(1024)S(1)} %copy-done.9), kind=kOutput, calls=%fused_computation.78 | convolution fusion | flops 8515190784 | bytes 54992896 | tf_op jit(solution)/shard_map/transpose(jvp())/dot_general | solution.py:21
  285.9 0.0 all-reduce.3.cloned.1.call-update
  286.0 485.9 %all-reduce.3.cloned.1.call-done = (bf16[1,896,2304]{2,1,0:T(8,128)(2,1)}, bf16[1,896,2304]{2,1,0:T(8,128)(2,1)}, bf16[1,896,2304]{2,1,0:T(8,128)(2,1)}, bf16[1,...) async-done(((bf16[1,896,2304]{2,1,0:T(8,128)(2,1)}, bf16[1,896,2304]{2,1,0:T(8,128)(2,1)}, bf16[1,896,2304]{2,1,0:T(8,128)(2,1)}, ...) | async-done | bytes 24772624 | tf_op jit(solution)/shard_map/psum | solution.py:45
  771.9 28.9 %fusion.21 = (bf16[2,2304,896]{2,1,0:T(8,128)(2,1)}, f32[2,2304,896]{2,1,0:T(8,128)}, f32[2,2304,896]{2,1,0:T(8,128)}) fusion(bf16[2,2304,896]{2,1,0:T(8,128)(2,1)} %param.15, bf16[1,2304,896]{2,1,0:T(8,128)(2,1)} %get-tuple-element.13, bf16[1,2304,896]{2,1,0:T(8,128)(2,1)} %get-tuple-element.14, f32[2,2304,896]{2,1,0:T(8,128)} %param.21, ...), kind=kLoop, calls=%fused_computation.42 | loop fusion | flops 78446592 | bytes 90832896 | tf_op jit(solution)/shard_map/convert_element_type | solution.py:30
  800.8 58.4 %fusion.13 = (bf16[2,896,2304]{2,1,0:T(8,128)(2,1)}, f32[2,896,2304]{2,1,0:T(8,128)}, f32[2,896,2304]{2,1,0:T(8,128)}, bf16[2,896,2304]{2,1,0:T(8,128)(2,1)}, f3...) fusion(bf16[2,896,2304]{2,1,0:T(8,128)(2,1)} %param.13, bf16[1,896,2304]{2,1,0:T(8,128)(2,1)} %get-tuple-element.9, ...), kind=kLoop, calls=%fused_computation.34 | loop fusion | flops 156893184 | bytes 181665792 | tf_op jit(solution)/shard_map/convert_element_type | solution.py:30
  (4 shorter events, 0.0 us)
Async XLA Ops:
  7.2 764.7 %all-reduce.3.cloned.1.call-start = ((), (), s32[]{:S(2)}) async-start(), calls=%async_computation | async-start | bytes 49545216 | tf_op jit(solution)/shard_map/psum | solution.py:45
  16.1 36.9 %copy-start.8 = (f32[2048]{0:T(1024)}, f32[2048]{0:T(1024)S(1)}, u32[]{:S(2)}) copy-start(f32[2048]{0:T(1024)S(1)} %add_rsqrt_fusion) | copy-start | bytes 24580
  22.3 15.2 %copy-start.2 = (bf16[1,2048,896]{2,1,0:T(8,128)(2,1)S(1)}, bf16[1,2048,896]{2,1,0:T(8,128)(2,1)}, u32[]{:S(2)}) copy-start(bf16[1,2048,896]{2,1,0:T(8,128)(2,1)} %param.11) | copy-start | bytes 11010052
  88.5 16.4 %copy-start.3 = (bf16[2048,896]{0,1:T(8,128)(2,1)}, bf16[2048,896]{0,1:T(8,128)(2,1)S(1)}, u32[]{:S(2)}) copy-start(bf16[2048,896]{0,1:T(8,128)(2,1)S(1)} %get-tuple-element.27) | copy-start | bytes 11010052
  88.5 16.4 %copy-start.6 = (f32[2048]{0:T(1024)}, f32[2048]{0:T(1024)S(1)}, u32[]{:S(2)}) copy-start(f32[2048]{0:T(1024)S(1)} %get-tuple-element.26) | copy-start | bytes 24580
  186.0 14.6 %copy-start.4 = (bf16[2048,896]{0,1:T(8,128)(2,1)S(1)}, bf16[2048,896]{0,1:T(8,128)(2,1)}, u32[]{:S(2)}) copy-start(bf16[2048,896]{0,1:T(8,128)(2,1)} %copy-done.3) | copy-start | bytes 11010052
  186.0 33.0 %slice-start = ((s8[8257536]{0:T(1024)(128)(4,1)}), s8[4194304]{0:T(1024)(128)(4,1)S(1)}, s32[]{:S(2)}) async-start(s8[8257536]{0:T(1024)(128)(4,1)} %bitcast.74), calls=%async_computation.1 | async-start | bytes 8388608
  200.6 13.8 %copy-start.7 = (f32[2048]{0:T(1024)S(1)}, f32[2048]{0:T(1024)}, u32[]{:S(2)}) copy-start(f32[2048]{0:T(1024)} %copy-done.6) | copy-start | bytes 24580
  200.6 13.8 %copy-start.1 = (bf16[1,2048,896]{1,2,0:T(8,128)(2,1)S(1)}, bf16[1,2048,896]{1,2,0:T(8,128)(2,1)}, u32[]{:S(2)}) copy-start(bf16[1,2048,896]{1,2,0:T(8,128)(2,1)} %copy.21) | copy-start | bytes 11010052
  200.6 18.5 %slice-start.1 = ((s8[8257536]{0:T(1024)(128)(4,1)}), s8[4063232]{0:T(1024)(128)(4,1)S(1)}, s32[]{:S(2)}) async-start(s8[8257536]{0:T(1024)(128)(4,1)} %bitcast.74), calls=%async_computation.2 | async-start | bytes 8126464
  219.1 14.6 %copy-start.5 = (bf16[2048,896]{0,1:T(8,128)(2,1)S(1)}, bf16[2048,896]{0,1:T(8,128)(2,1)}, u32[]{:S(2)}) copy-start(bf16[2048,896]{0,1:T(8,128)(2,1)} %fusion.70) | copy-start | bytes 11010052
  233.7 14.1 %copy-start = (bf16[1,2048,896]{1,2,0:T(8,128)(2,1)S(1)}, bf16[1,2048,896]{1,2,0:T(8,128)(2,1)}, u32[]{:S(2)}) copy-start(bf16[1,2048,896]{1,2,0:T(8,128)(2,1)} %copy.20) | copy-start | bytes 11010052
  233.7 14.1 %copy-start.9 = (f32[2048]{0:T(1024)S(1)}, f32[2048]{0:T(1024)}, u32[]{:S(2)}) copy-start(f32[2048]{0:T(1024)} %copy-done.8) | copy-start | bytes 24580
Sparse Core Ops, SparseCore 0:
  286.1 485.7 all-reduce.2
where the time goes:
time: 874 us; the launch traced here: 866 us
  waiting for transfers between devices  486 us (56%)
  matrix products  259 us (30%)
  other arithmetic  94.8 us (11%)
  between operations  14.3 us (2%)
  local copies, waits for them, and re-layouts  12.3 us (1%)
    psum x1, waiting for transfers between devices, step(): summed[number] = [lax.psum(by_w[name], 'dp') for name in NAMES]  486 us
    dot_general x5, matrix products, layer(): gate = jnp.dot(a, w['w_gate'], preferred_element_type=jnp.float32)  91 us
    dot_general x5, matrix products, layer(): up = jnp.dot(a, w['w_up'], preferred_element_type=jnp.float32)  90.4 us
    convert_element_type x2, other arithmetic, adamw(): return ((w - 0.02 * step).astype(jnp.bfloat16), m, v)  87.3 us
    dot_general x5, matrix products, matmul(): jnp.dot(a, w, preferred_element_type=jnp.float32).astype(jnp.bfloat16)  77.5 us
  transfers between devices with their start and end apart: 1, of which 1 were waited for; matrix products, arithmetic and copies ran while one was open for 0% of the time, Pallas kernels for 0%

commit v1 on v0

v1 whole, which is shorter than its diff:
```python
import functools
import jax, jax.numpy as jnp
from jax import lax
from jax.experimental import pallas as pl
from jax.experimental.pallas import tpu as pltpu
BF, F32 = jnp.bfloat16, jnp.float32
T, D, FF = 2048, 896, 2304
C = 256
NCH = FF // C
HALF = 3 * D // 2
VL = 60 * 2**20
NT = (((1,), (1,)), ((), ()))

def dot(a, b, dims=(((1,), (0,)), ((), ()))):
    return lax.dot_general(a, b, dims, preferred_element_type=F32)

def cparams(**kw):
    return pltpu.CompilerParams(vmem_limit_bytes=VL, **kw)

VM = pl.BlockSpec(memory_space=pltpu.VMEM)
ANY = pl.BlockSpec(memory_space=pl.ANY)

def norm_scale(wide):
    return lax.rsqrt(jnp.mean(wide * wide, -1, keepdims=True) + 1e-6)

def fwd_body(x_hbm, dy_hbm, wg_ref, wu_ref, wd_hbm, h_hbm, a1_hbm, a1t_hbm, a0_hbm, a0t_hbm, dyt_hbm,
             x, dy, a0, a0t, dyt, hid, wd, h, a1, a1t, sem):
    j = pl.program_id(0)
    RT = 512
    def cin(src, dst, i): return pltpu.make_async_copy(src, dst, sem.at[i])
    def rows(i): return pl.ds(i * RT, RT)
    outs = lambda: [cin(a0, a0_hbm, 4), cin(a0t, a0t_hbm, 5), cin(dyt, dyt_hbm, 6)]
    @pl.when(j == 0)
    def _():
        for i in range(4):
            cin(x_hbm.at[rows(i)], x.at[rows(i)], 12 + i).start()
        cin(dy_hbm, dy, 1).start()
        cin(wd_hbm.at[0], wd, 2).start()
        for i in range(4):
            cin(x_hbm.at[rows(i)], x.at[rows(i)], 12 + i).wait()
            wide = x[rows(i), :].astype(F32)
            a = (wide * norm_scale(wide)).astype(BF)
            a0[rows(i), :] = a
            a0t[:, rows(i)] = a.T
        cin(dy_hbm, dy, 1).wait()
        for i in range(4):
            dyt[:, rows(i)] = dy[rows(i), :].T
        for c in outs(): c.start()
    cols = pl.ds(pl.multiple_of(j * C, C), C)
    for i in range(4):
        a = a0[rows(i), :]
        g = dot(a, wg_ref[0]); u = dot(a, wu_ref[0])
        hid[rows(i), cols] = (g * jax.nn.sigmoid(g) * u).astype(BF)
    @pl.when(j == NCH - 1)
    def _():
        cin(wd_hbm.at[0], wd, 2).wait()
        cs = []
        for i in range(8):
            r = pl.ds(i * 256, 256)
            o = dot(hid[r, :], wd[...]).astype(BF)
            y = x[r, :] + o
            h[r, :] = y
            wide = y.astype(F32)
            a = (wide * norm_scale(wide)).astype(BF)
            a1[r, :] = a
            a1t[:, r] = a.T
            if i % 2:
                rr = rows(i // 2)
                new = [cin(h.at[rr], h_hbm.at[rr], 16 + 2 * i), cin(a1.at[rr], a1_hbm.at[rr], 17 + 2 * i)]
                for c in new: c.start()
                cs += new
        c = cin(a1t, a1t_hbm, 3); c.start(); cs.append(c)
        for c in outs() + cs: c.wait()

def fwd(x, dy, wg, wu, wd):
    s = jax.ShapeDtypeStruct((T, D), BF); st = jax.ShapeDtypeStruct((D, T), BF)
    v = pltpu.VMEM((T, D), BF); vt = pltpu.VMEM((D, T), BF)
    return pl.pallas_call(
        fwd_body, grid=(NCH,), name="fwd0",
        out_shape=(s, s, st, s, st, st),
        in_specs=[ANY, ANY, pl.BlockSpec((1, D, C), lambda j: (0, 0, j)), pl.BlockSpec((1, D, C), lambda j: (0, 0, j)), ANY],
        out_specs=[ANY] * 6,
        scratch_shapes=[v, v, v, vt, vt, pltpu.VMEM((T, FF), BF), pltpu.VMEM((FF, D), BF), v, v, vt, pltpu.SemaphoreType.DMA((32,))],
        compiler_params=cparams(dimension_semantics=("arbitrary",)),
    )(x, dy, wg, wu, wd)

U = 2 * NCH
NR2 = 9
STAGE2 = (3, 5, 6, 8, 9, 11, 13, 15, 17)
STAGE3 = (5, 7, 9, 10, 12, 14, 16)
STAGE4 = (7, 9, 12, 14, 16)
MESH = pl.DeviceIdType.MESH

def upto(table, s):
    n = jnp.int32(0)
    for t in table:
        n = n + jnp.where(s >= t, 1, 0)
    return n

def mega_body(a1_hbm, a1t_hbm, dy_hbm, dyt_hbm, h1_hbm, a0_hbm, a0t_hbm, wg_ref, wu_ref, wd_ref, f_hbm,
              a, at, d, dt, acc, hid, dg, du, buf, r0, r1, r2,
              sem, p0s, p0r, s1s, s1r, ms, mr, os_, or_, ps, pr, lf, free):
    s = pl.program_id(0)
    me = lax.axis_index("dp")
    core, z = lax.rem(me, 2), lax.div(me, 2)
    inner = jnp.logical_and(z >= 1, z <= 2)
    outer = jnp.logical_not(inner)
    partner = me + 1 - 2 * core
    up = me + 2 - 4 * lax.div(z, 3)
    mid = me + 6 - 4 * z
    out = me - 6 + 4 * z
    RT = 512

    def local(src, dst, i): return pltpu.make_async_copy(src, dst, sem.at[i])
    def remote(src, dst, ss, rs, dev):
        return pltpu.make_async_remote_copy(src_ref=src, dst_ref=dst, send_sem=ss, recv_sem=rs, device_id={"dp": dev}, device_id_type=MESH)
    def rows(i): return pl.ds(i * RT, RT)

    def cp0(u): return remote(buf.at[lax.rem(u, 2), 1 - core], r0.at[u], p0s.at[u], p0r.at[u], partner)
    def cs1(u): return remote(r0.at[u], r1.at[u], s1s.at[u], s1r.at[u], up)
    def cmid(u): return remote(r0.at[u], r2.at[lax.rem(u, NR2)], ms.at[u], mr.at[u], mid)
    def cout(u): return remote(r1.at[u], f_hbm.at[u, core], os_.at[u], or_.at[u], out)
    def cp4i(u): return remote(r1.at[u], f_hbm.at[u, core], ps.at[u], pr.at[u], partner)
    def cp4o(u): return remote(f_hbm.at[u, core], f_hbm.at[u, core], ps.at[u], pr.at[u], partner)
    def clf(u): return pltpu.make_async_copy(r1.at[u], f_hbm.at[u, core], lf.at[u])

    def plus(dst, x, y):
        def part(k, c):
            r = pl.ds(pl.multiple_of(k * 224, 32), 224)
            dst[r, :] = (x[r, :].astype(F32) + y[r, :].astype(F32)).astype(BF)
            return c
        lax.fori_loop(0, 6, part, 0)

    def stage1(u):
        c = cp0(u)
        c.wait()
        plus(r0.at[u], r0.at[u], buf.at[lax.rem(u, 2), core])
        @pl.when(outer)
        def _(): cs1(u).start()

    def stage2(u, c=0):
        cs1(u).wait_recv()
        plus(r0.at[u], r0.at[u], r1.at[u])
        @pl.when(u >= NR2)
        def _(): pl.semaphore_wait(free, 1)
        cmid(u).start()
        return c

    def stage3(u, c=0):
        cmid(u).wait_recv()
        plus(r1.at[u], r0.at[u], r2.at[lax.rem(u, NR2)])
        @pl.when(u < U - NR2)
        def _(): pl.semaphore_signal(free, inc=1, device_id={"dp": mid}, device_id_type=MESH)
        cout(u).start()
        cp4i(u).start()
        clf(u).start()
        return c

    def stage4(u, c=0):
        cout(u).wait_recv()
        cp4o(u).start()
        return c

    @pl.when(s == 0)
    def _():
        barrier = pltpu.get_barrier_semaphore()
        pl.semaphore_signal(barrier, inc=1, device_id={"dp": partner}, device_id_type=MESH)
        @pl.when(outer)
        def _():
            pl.semaphore_signal(barrier, inc=1, device_id={"dp": up}, device_id_type=MESH)
            pl.semaphore_wait(barrier, 2)
        @pl.when(inner)
        def _():
            pl.semaphore_signal(barrier, inc=1, device_id={"dp": mid}, device_id_type=MESH)
            pl.semaphore_signal(barrier, inc=1, device_id={"dp": out}, device_id_type=MESH)
            pl.semaphore_wait(barrier, 3)
        cs = [local(x, y, i) for i, (x, y) in enumerate(((a1_hbm, a), (dy_hbm, d), (a1t_hbm, at), (dyt_hbm, dt)))]
        for c in cs: c.start()
        acc[...] = jnp.zeros((T, D), F32)
        for c in cs: c.wait()

    @pl.when(s == NCH)
    def _():
        local(h1_hbm, a, 0).start()
        local(a0t_hbm, at, 2).start()
        local(h1_hbm, a, 0).wait()
        def part(i, c):
            r = pl.ds(pl.multiple_of(i * 256, 256), 256)
            g = acc[r, :].astype(BF).astype(F32)
            wide = a[r, :].astype(F32)
            scale = norm_scale(wide)
            n = wide * scale
            v = d[r, :] + (scale * (g - n * jnp.mean(n * g, -1, keepdims=True))).astype(BF)
            d[r, :] = v
            dt[:, r] = v.T
            return c
        lax.fori_loop(0, T // 256, part, 0)
        local(a0_hbm, a, 1).start()
        local(a0t_hbm, at, 2).wait()
        local(a0_hbm, a, 1).wait()

    for i in range(T // RT):
        r = rows(i)
        g = dot(a[r, :], wg_ref[0]); u = dot(a[r, :], wu_ref[0])
        dh = dot(d[r, :], wd_ref[0], NT).astype(BF).astype(F32)
        sg = jax.nn.sigmoid(g)
        sl = g * sg
        hid[r, :] = (sl * u).astype(BF)
        du[r, :] = (dh * sl).astype(BF)
        dg[r, :] = (dh * u * (sg + sl * (1 - sg))).astype(BF)

    @pl.when(s >= 1)
    def _(): stage1(s - 1)
    @pl.when(inner)
    def _():
        lax.fori_loop(upto(STAGE2, s - 1), upto(STAGE2, s), stage2, 0)
        lax.fori_loop(upto(STAGE3, s - 1), upto(STAGE3, s), stage3, 0)
    @pl.when(outer)
    def _():
        lax.fori_loop(upto(STAGE4, s - 1), upto(STAGE4, s), stage4, 0)

    slot = lax.rem(s, 2)
    for tile in range(6):
        lhs, rhs = ((at, dg), (at, du), (dt, hid))[tile // 2]
        half, k = divmod(tile, 3)
        buf[slot, half, pl.ds(k * 448, 448), :] = dot(lhs[pl.ds(tile % 2 * 448, 448), :], rhs[...]).astype(BF)
    cp0(s).start()

    @pl.when(s < NCH)
    def _():
        def part(i, c):
            r = pl.ds(pl.multiple_of(i * RT, RT), RT)
            acc[r, :] += dot(dg[r, :], wg_ref[0], NT) + dot(du[r, :], wu_ref[0], NT)
            return c
        lax.fori_loop(0, T // RT, part, 0)

    @pl.when(s == U - 1)
    def _():
        stage1(s)
        @pl.when(inner)
        def _():
            n2, n3 = len(STAGE2), len(STAGE3)
            def both(u, c):
                stage2(u)
                return stage3(u - (n2 - n3), c)
            lax.fori_loop(n2, U, both, 0)
            lax.fori_loop(U - (n2 - n3), U, stage3, 0)
            def done(u, c):
                cmid(u).wait_send(); cout(u).wait_send(); clf(u).wait()
                cp4i(u).wait_send(); cp4i(u).wait_recv()
                return c
            lax.fori_loop(0, U, done, 0)
        @pl.when(outer)
        def _():
            lax.fori_loop(len(STAGE4), U, stage4, 0)
            def done(u, c):
                cs1(u).wait_send()
                cp4o(u).wait_send(); cp4o(u).wait_recv()
                return c
            lax.fori_loop(0, U, done, 0)

def mega(a1, a1t, dy, dyt, h1, a0, a0t, wg, wu, wd):
    v = pltpu.VMEM((T, D), BF); vt = pltpu.VMEM((D, T), BF); w = pltpu.VMEM((T, C), BF)
    up = pl.BlockSpec((1, D, C), lambda s: (1 - s // NCH, 0, s % NCH)); dn = pl.BlockSpec((1, C, D), lambda s: (1 - s // NCH, s % NCH, 0))
    q = lambda n: pltpu.VMEM((n, HALF, C), BF)
    sems = pltpu.SemaphoreType.DMA((U,))
    return pl.pallas_call(
        mega_body, grid=(U,), name="backward",
        out_shape=jax.ShapeDtypeStruct((U, 2, HALF, C), BF),
        in_specs=[ANY] * 7 + [up, up, dn], out_specs=ANY,
        scratch_shapes=[v, vt, v, vt, pltpu.VMEM((T, D), F32), w, w, w, pltpu.VMEM((2, 2, HALF, C), BF), q(U), q(U), q(NR2),
                        pltpu.SemaphoreType.DMA((4,))] + [sems] * 11 + [pltpu.SemaphoreType.REGULAR],
        compiler_params=pltpu.CompilerParams(vmem_limit_bytes=67043328, dimension_semantics=("arbitrary",), collective_id=0, has_side_effects=True),
    )(a1, a1t, dy, dyt, h1, a0, a0t, wg, wu, wd)

def adamw(w, m, v, g):
    m = 0.9 * m + 0.1 * g
    v = 0.95 * v + 0.05 * g * g
    step = m * lax.rsqrt(v + 1e-8) + 0.1 * w
    return (w - 0.02 * step).astype(BF), m, v

def adam_body(f_ref, *refs):
    ins, outs = refs[:9], refs[9:]
    lo, hi = f_ref[0, 0].astype(F32), f_ref[0, 1].astype(F32)
    gs = (lo[:D], jnp.concatenate([lo[D:], hi[:HALF - D]], 0), hi[HALF - D:].T)
    for k, g in enumerate(gs):
        w, m, v = adamw(ins[k][0].astype(F32), ins[3 + k][0], ins[6 + k][0], g)
        outs[k][0] = w; outs[3 + k][0] = m; outs[6 + k][0] = v

def adam(f, args9):
    up = pl.BlockSpec((1, D, C), lambda s: (1 - s // NCH, 0, s % NCH)); dn = pl.BlockSpec((1, C, D), lambda s: (1 - s // NCH, s % NCH, 0))
    dts = [BF] * 3 + [F32] * 6
    return pl.pallas_call(
        adam_body, grid=(U,), name="adam",
        in_specs=[pl.BlockSpec((1, 2, HALF, C), lambda s: (s, 0, 0, 0))] + [up, up, dn] * 3, out_specs=[up, up, dn] * 3,
        out_shape=[jax.ShapeDtypeStruct((2, FF, D) if k % 3 == 2 else (2, D, FF), dts[k]) for k in range(9)],
        compiler_params=cparams(dimension_semantics=("arbitrary",)),
    )(f, *args9)

from jax.sharding import PartitionSpec as P

def solution(mesh):
    def step(x, dy, *arrays):
        wg, wu, wd = arrays[:3]
        x, dy = x[0], dy[0]
        h1, a1, a1t, a0, a0t, dyt = fwd(x, dy, wg, wu, wd)
        f = mega(a1, a1t, dy, dyt, h1, a0, a0t, wg, wu, wd)
        return tuple(adam(f, arrays))

    return jax.shard_map(
        step,
        mesh=mesh,
        in_specs=(P(("rep", "dp"), None, None),) * 2 + (P(None, None, None),) * 9,
        out_specs=(P("rep", None, None),) * 9,
        check_vma=False,
    )
```

time: 874 us -> 482 us (0.55)
  waiting for transfers between devices: 486 us -> 0 us
  Pallas kernels: 0 us -> 481 us
  matrix products: 259 us -> 0 us
  other arithmetic: 94.8 us -> 0 us
  between operations: 14.3 us -> 0.82 us
  local copies, waits for them, and re-layouts: 12.3 us -> 0 us
    psum x1 -> x0, waiting for transfers between devices: 486 us -> none  [step(): summed[number] = [lax.psum(by_w[name], 'dp') for name in NAMES]]
    pallas_call x0 -> x3, Pallas kernels: none -> 481 us  [the longest x1 353 us: mega(): pl.pallas_call(mega_body, grid=(U,), name='backward', out_shape=jax.Shape...]
    dot_general x15 -> x0, matrix products: 259 us -> none  [the longest x5 91 us: layer(): gate = jnp.dot(a, w['w_gate'], preferred_element_type=jnp.float32)]
    convert_element_type x2 -> x0, other arithmetic: 87.3 us -> none  [adamw(): return ((w - 0.02 * step).astype(jnp.bfloat16), m, v)]
    unnamed x26 -> x0, local copies, waits for them, and re-layouts: 12.3 us -> none
  transfers between devices with their start and end apart: 1 -> 0, of which waited for: 1 -> 0; matrix products, arithmetic and copies ran while one was open for 0% -> 0% of each run, Pallas kernels for 0% -> 0%
where the time goes in v1:
time: 482 us
  Pallas kernels  481 us (100%)
    pallas_call x1, Pallas kernels, mega(): pl.pallas_call(mega_body, grid=(U,), name='backward', out_shape=jax.Shape...  353 us
    pallas_call x1, Pallas kernels, adam(): pl.pallas_call(adam_body, grid=(U,), name='adam', in_specs=[pl.BlockSpec(...  88.6 us
    pallas_call x1, Pallas kernels, fwd(): pl.pallas_call(fwd_body, grid=(NCH,), name='fwd0', out_shape=(s, s, st, s...  40 us

profile of v1, /device:TPU:0, one launch (start us, length us, event | category | flops | bytes accessed | tf_op | source)
XLA Modules:
  0.0 482.0 jit_solution(12039917154351816195)
XLA Ops:
  0.6 40.0 %fwd0.1 = (bf16[2048,896]{1,0:T(8,128)(2,1)}, bf16[2048,896]{1,0:T(8,128)(2,1)}, bf16[896,2048]{1,0:T(8,128)(2,1)}, bf16[2048,896]{1,0:T(8,128)(2,1)}, bf16[896,...) custom-call(bf16[2048,896]{1,0:T(8,128)(2,1)} %bitcast.4, bf16[2048,896]{1,0:T(8,128)(2,1)} %bitcast.2, ...), custom_call_target="tpu_custom_call" | custom-call | tf_op jit(solution)/shard_map/fwd0/pallas_call | solution.py:78
  40.7 352.6 %backward.1.f_ref = bf16[18,2,1344,256]{3,2,1,0:T(8,128)(2,1)} custom-call(bf16[2048,896]{1,0:T(8,128)(2,1)} %get-tuple-element.15.a1_hbm, bf16[896,2048]{1,0:T(8,128)(2,1)} %get-tuple-element.16.a1t_hbm, bf16[2048,896]{1,0:T(8,128)(2,1)} %bitcast.3, bf16[896,2048]{1,0:T(8,128)(2,1)} %get-tuple-element.17.dyt_hbm, ...), custom_call_target="tpu_custom_call" | custom-call | tf_op jit(solution)/shard_map/backward/pallas_call | solution.py:267
  393.3 88.6 %adam.1 = (bf16[2,896,2304]{2,1,0:T(8,128)(2,1)}, bf16[2,896,2304]{2,1,0:T(8,128)(2,1)}, bf16[2,2304,896]{2,1,0:T(8,128)(2,1)}, f32[2,896,2304]{2,1,0:T(8,128)},...) custom-call(bf16[18,2,1344,256]{3,2,1,0:T(8,128)(2,1)} %backward.1.f, ...), custom_call_target="tpu_custom_call" | custom-call | tf_op jit(solution)/shard_map/adam/pallas_call | solution.py:293

commit v2 on v1

--- a/solution.py
+++ b/solution.py
@@ -39,20 +39,20 @@
         for i in range(4):
             cin(x_hbm.at[rows(i)], x.at[rows(i)], 12 + i).wait()
             wide = x[rows(i), :].astype(F32)
-            a = (wide * norm_scale(wide)).astype(BF)
-            a0[rows(i), :] = a
-            a0t[:, rows(i)] = a.T
+            a0[rows(i), :] = (wide * norm_scale(wide)).astype(BF)
+        cin(a0, a0_hbm, 4).start()
         cin(dy_hbm, dy, 1).wait()
-        for i in range(4):
-            dyt[:, rows(i)] = dy[rows(i), :].T
-        for c in outs(): c.start()
     cols = pl.ds(pl.multiple_of(j * C, C), C)
     for i in range(4):
         a = a0[rows(i), :]
         g = dot(a, wg_ref[0]); u = dot(a, wu_ref[0])
         hid[rows(i), cols] = (g * jax.nn.sigmoid(g) * u).astype(BF)
+    r = pl.ds(pl.multiple_of(jnp.minimum(j, 7) * 256, 256), 256)
+    a0t[:, r] = a0[r, :].T
+    dyt[:, r] = dy[r, :].T
     @pl.when(j == NCH - 1)
     def _():
+        for c in outs()[1:]: c.start()
         cin(wd_hbm.at[0], wd, 2).wait()
         cs = []
         for i in range(8):
@@ -85,10 +85,12 @@
     )(x, dy, wg, wu, wd)
 
 U = 2 * NCH
-NR2 = 9
-STAGE2 = (3, 5, 6, 8, 9, 11, 13, 15, 17)
-STAGE3 = (5, 7, 9, 10, 12, 14, 16)
-STAGE4 = (7, 9, 12, 14, 16)
+V = 2 * U
+SUB = HALF // 2
+NR2 = 18
+STAGE2 = (2, 3, 3, 4, 5, 5, 6, 7, 7, 8, 9, 9, 9, 10, 11, 12, 13, 14, 14, 15, 16, 17)
+STAGE3 = (4, 4, 5, 6, 6, 7, 8, 8, 9, 10, 10, 10, 11, 12, 13, 14, 15, 15, 16, 17)
+STAGE4 = (5, 6, 7, 7, 8, 9, 9, 10, 11, 11, 11, 12, 13, 14, 15, 16, 16, 17)
 MESH = pl.DeviceIdType.MESH
 
 def upto(table, s):
@@ -116,31 +118,38 @@
         return pltpu.make_async_remote_copy(src_ref=src, dst_ref=dst, send_sem=ss, recv_sem=rs, device_id={"dp": dev}, device_id_type=MESH)
     def rows(i): return pl.ds(i * RT, RT)
 
-    def cp0(u): return remote(buf.at[lax.rem(u, 2), 1 - core], r0.at[u], p0s.at[u], p0r.at[u], partner)
-    def cs1(u): return remote(r0.at[u], r1.at[u], s1s.at[u], s1r.at[u], up)
-    def cmid(u): return remote(r0.at[u], r2.at[lax.rem(u, NR2)], ms.at[u], mr.at[u], mid)
-    def cout(u): return remote(r1.at[u], f_hbm.at[u, core], os_.at[u], or_.at[u], out)
-    def cp4i(u): return remote(r1.at[u], f_hbm.at[u, core], ps.at[u], pr.at[u], partner)
-    def cp4o(u): return remote(f_hbm.at[u, core], f_hbm.at[u, core], ps.at[u], pr.at[u], partner)
-    def clf(u): return pltpu.make_async_copy(r1.at[u], f_hbm.at[u, core], lf.at[u])
-
-    def plus(dst, x, y):
+    def cp0(u): return remote(buf.at[lax.rem(u, 2), 1 - core], r0.at[pl.ds(pl.multiple_of(u * HALF, HALF), HALF)], p0s.at[u], p0r.at[u], partner)
+    def at0(p): return r0.at[pl.ds(pl.multiple_of(p * SUB, SUB), SUB)]
+    def at1(p): return r1.at[pl.ds(pl.multiple_of(p * SUB, SUB), SUB)]
+    def at2(p): return r2.at[pl.ds(pl.multiple_of(lax.rem(p, NR2) * SUB, SUB), SUB)]
+    def to(p): return f_hbm.at[lax.div(p, 2), core, pl.ds(pl.multiple_of(lax.rem(p, 2) * SUB, SUB), SUB)]
+    def cs1(p): return remote(at0(p), at1(p), s1s.at[p], s1r.at[p], up)
+    def cmid(p): return remote(at0(p), at2(p), ms.at[p], mr.at[p], mid)
+    def cout(p): return remote(at1(p), to(p), os_.at[p], or_.at[p], out)
+    def cp4i(p): return remote(at1(p), to(p), ps.at[p], pr.at[p], partner)
+    def cp4o(p): return remote(to(p), to(p), ps.at[p], pr.at[p], partner)
+    def clf(p): return pltpu.make_async_copy(at1(p), to(p), lf.at[p])
+
+    def plus(dst, x, y, n):
         def part(k, c):
             r = pl.ds(pl.multiple_of(k * 224, 32), 224)
             dst[r, :] = (x[r, :].astype(F32) + y[r, :].astype(F32)).astype(BF)
             return c
-        lax.fori_loop(0, 6, part, 0)
+        lax.fori_loop(0, n, part, 0)
 
     def stage1(u):
         c = cp0(u)
         c.wait()
-        plus(r0.at[u], r0.at[u], buf.at[lax.rem(u, 2), core])
+        whole = r0.at[pl.ds(pl.multiple_of(u * HALF, HALF), HALF)]
+        plus(whole, whole, buf.at[lax.rem(u, 2), core], 6)
         @pl.when(outer)
-        def _(): cs1(u).start()
+        def _():
+            cs1(2 * u).start()
+            cs1(2 * u + 1).start()
 
     def stage2(u, c=0):
         cs1(u).wait_recv()
-        plus(r0.at[u], r0.at[u], r1.at[u])
+        plus(at0(u), at0(u), at1(u), 3)
         @pl.when(u >= NR2)
         def _(): pl.semaphore_wait(free, 1)
         cmid(u).start()
@@ -148,8 +157,8 @@
 
     def stage3(u, c=0):
         cmid(u).wait_recv()
-        plus(r1.at[u], r0.at[u], r2.at[lax.rem(u, NR2)])
-        @pl.when(u < U - NR2)
+        plus(at1(u), at0(u), at2(u), 3)
+        @pl.when(u < V - NR2)
         def _(): pl.semaphore_signal(free, inc=1, device_id={"dp": mid}, device_id_type=MESH)
         cout(u).start()
         cp4i(u).start()
@@ -177,7 +186,7 @@
         cs = [local(x, y, i) for i, (x, y) in enumerate(((a1_hbm, a), (dy_hbm, d), (a1t_hbm, at), (dyt_hbm, dt)))]
         for c in cs: c.start()
         acc[...] = jnp.zeros((T, D), F32)
-        for c in cs: c.wait()
+        for c in cs[:2]: c.wait()
 
     @pl.when(s == NCH)
     def _():
@@ -209,7 +218,11 @@
         du[r, :] = (dh * sl).astype(BF)
         dg[r, :] = (dh * u * (sg + sl * (1 - sg))).astype(BF)
 
-    @pl.when(s >= 1)
+    @pl.when(s == 0)
+    def _():
+        local(a1t_hbm, at, 2).wait()
+        local(dyt_hbm, dt, 3).wait()
+    @pl.when(s > NCH)
     def _(): stage1(s - 1)
     @pl.when(inner)
     def _():
@@ -233,6 +246,7 @@
             acc[r, :] += dot(dg[r, :], wg_ref[0], NT) + dot(du[r, :], wu_ref[0], NT)
             return c
         lax.fori_loop(0, T // RT, part, 0)
+        stage1(s)
 
     @pl.when(s == U - 1)
     def _():
@@ -240,35 +254,36 @@
         @pl.when(inner)
         def _():
             n2, n3 = len(STAGE2), len(STAGE3)
+            lax.fori_loop(n3, n2 - 1, stage3, 0)
             def both(u, c):
                 stage2(u)
-                return stage3(u - (n2 - n3), c)
-            lax.fori_loop(n2, U, both, 0)
-            lax.fori_loop(U - (n2 - n3), U, stage3, 0)
+                return stage3(u - 1, c)
+            lax.fori_loop(n2, V, both, 0)
+            stage3(V - 1)
             def done(u, c):
                 cmid(u).wait_send(); cout(u).wait_send(); clf(u).wait()
                 cp4i(u).wait_send(); cp4i(u).wait_recv()
                 return c
-            lax.fori_loop(0, U, done, 0)
+            lax.fori_loop(0, V, done, 0)
         @pl.when(outer)
         def _():
-            lax.fori_loop(len(STAGE4), U, stage4, 0)
+            lax.fori_loop(len(STAGE4), V, stage4, 0)
             def done(u, c):
                 cs1(u).wait_send()
                 cp4o(u).wait_send(); cp4o(u).wait_recv()
                 return c
-            lax.fori_loop(0, U, done, 0)
+            lax.fori_loop(0, V, done, 0)
 
 def mega(a1, a1t, dy, dyt, h1, a0, a0t, wg, wu, wd):
     v = pltpu.VMEM((T, D), BF); vt = pltpu.VMEM((D, T), BF); w = pltpu.VMEM((T, C), BF)
     up = pl.BlockSpec((1, D, C), lambda s: (1 - s // NCH, 0, s % NCH)); dn = pl.BlockSpec((1, C, D), lambda s: (1 - s // NCH, s % NCH, 0))
-    q = lambda n: pltpu.VMEM((n, HALF, C), BF)
-    sems = pltpu.SemaphoreType.DMA((U,))
+    q = lambda n: pltpu.VMEM((n * SUB, C), BF)
+    sems = pltpu.SemaphoreType.DMA((V,))
     return pl.pallas_call(
         mega_body, grid=(U,), name="backward",
         out_shape=jax.ShapeDtypeStruct((U, 2, HALF, C), BF),
         in_specs=[ANY] * 7 + [up, up, dn], out_specs=ANY,
-        scratch_shapes=[v, vt, v, vt, pltpu.VMEM((T, D), F32), w, w, w, pltpu.VMEM((2, 2, HALF, C), BF), q(U), q(U), q(NR2),
+        scratch_shapes=[v, vt, v, vt, pltpu.VMEM((T, D), F32), w, w, w, pltpu.VMEM((2, 2, HALF, C), BF), q(V), q(V), q(NR2),
                         pltpu.SemaphoreType.DMA((4,))] + [sems] * 11 + [pltpu.SemaphoreType.REGULAR],
         compiler_params=pltpu.CompilerParams(vmem_limit_bytes=67043328, dimension_semantics=("arbitrary",), collective_id=0, has_side_effects=True),
     )(a1, a1t, dy, dyt, h1, a0, a0t, wg, wu, wd)

time: 482 us -> 456 us (0.946)
  Pallas kernels: 481 us -> 455 us
    pallas_call x1, Pallas kernels: 353 us -> 328 us  [mega(): pl.pallas_call(mega_body, grid=(U,), name='backward', out_shape=jax.Shape...]
where the time goes in v2:
time: 456 us
  Pallas kernels  455 us (100%)
    pallas_call x1, Pallas kernels, mega(): pl.pallas_call(mega_body, grid=(U,), name='backward', out_shape=jax.Shape...  328 us
    pallas_call x1, Pallas kernels, adam(): pl.pallas_call(adam_body, grid=(U,), name='adam', in_specs=[pl.BlockSpec(...  88.6 us
    pallas_call x1, Pallas kernels, fwd(): pl.pallas_call(fwd_body, grid=(NCH,), name='fwd0', out_shape=(s, s, st, s...  38.8 us

profile of v2, /device:TPU:0, one launch (start us, length us, event | category | flops | bytes accessed | tf_op | source)
XLA Modules:
  0.0 455.7 jit_solution(14860875554594436036)
XLA Ops:
  0.6 38.8 %fwd0.1 = (bf16[2048,896]{1,0:T(8,128)(2,1)}, bf16[2048,896]{1,0:T(8,128)(2,1)}, bf16[896,2048]{1,0:T(8,128)(2,1)}, bf16[2048,896]{1,0:T(8,128)(2,1)}, bf16[896,...) custom-call(bf16[2048,896]{1,0:T(8,128)(2,1)} %bitcast.4, bf16[2048,896]{1,0:T(8,128)(2,1)} %bitcast.2, ...), custom_call_target="tpu_custom_call" | custom-call | tf_op jit(solution)/shard_map/fwd0/pallas_call | solution.py:78
  39.4 327.5 %backward.1.f_ref = bf16[18,2,1344,256]{3,2,1,0:T(8,128)(2,1)} custom-call(bf16[2048,896]{1,0:T(8,128)(2,1)} %get-tuple-element.15.a1_hbm, bf16[896,2048]{1,0:T(8,128)(2,1)} %get-tuple-element.16.a1t_hbm, bf16[2048,896]{1,0:T(8,128)(2,1)} %bitcast.3, bf16[896,2048]{1,0:T(8,128)(2,1)} %get-tuple-element.17.dyt_hbm, ...), custom_call_target="tpu_custom_call" | custom-call | tf_op jit(solution)/shard_map/backward/pallas_call | solution.py:282
  367.0 88.6 %adam.1 = (bf16[2,896,2304]{2,1,0:T(8,128)(2,1)}, bf16[2,896,2304]{2,1,0:T(8,128)(2,1)}, bf16[2,2304,896]{2,1,0:T(8,128)(2,1)}, f32[2,896,2304]{2,1,0:T(8,128)},...) custom-call(bf16[18,2,1344,256]{3,2,1,0:T(8,128)(2,1)} %backward.1.f, ...), custom_call_target="tpu_custom_call" | custom-call | tf_op jit(solution)/shard_map/adam/pallas_call | solution.py:308

commit v3 on v2

--- a/solution.py
+++ b/solution.py
@@ -7,6 +7,8 @@
 T, D, FF = 2048, 896, 2304
 C = 256
 NCH = FF // C
+CF = 768
+NF = FF // CF
 HALF = 3 * D // 2
 VL = 60 * 2**20
 NT = (((1,), (1,)), ((), ()))
@@ -42,15 +44,16 @@
             a0[rows(i), :] = (wide * norm_scale(wide)).astype(BF)
         cin(a0, a0_hbm, 4).start()
         cin(dy_hbm, dy, 1).wait()
-    cols = pl.ds(pl.multiple_of(j * C, C), C)
+    cols = pl.ds(pl.multiple_of(j * CF, CF), CF)
     for i in range(4):
         a = a0[rows(i), :]
         g = dot(a, wg_ref[0]); u = dot(a, wu_ref[0])
         hid[rows(i), cols] = (g * jax.nn.sigmoid(g) * u).astype(BF)
-    r = pl.ds(pl.multiple_of(jnp.minimum(j, 7) * 256, 256), 256)
-    a0t[:, r] = a0[r, :].T
-    dyt[:, r] = dy[r, :].T
-    @pl.when(j == NCH - 1)
+        if i < 3:
+            r = pl.ds(pl.multiple_of(jnp.minimum(j * 3 + i, 7) * 256, 256), 256)
+            a0t[:, r] = a0[r, :].T
+            dyt[:, r] = dy[r, :].T
+    @pl.when(j == NF - 1)
     def _():
         for c in outs()[1:]: c.start()
         cin(wd_hbm.at[0], wd, 2).wait()
@@ -76,9 +79,9 @@
     s = jax.ShapeDtypeStruct((T, D), BF); st = jax.ShapeDtypeStruct((D, T), BF)
     v = pltpu.VMEM((T, D), BF); vt = pltpu.VMEM((D, T), BF)
     return pl.pallas_call(
-        fwd_body, grid=(NCH,), name="fwd0",
+        fwd_body, grid=(NF,), name="fwd0",
         out_shape=(s, s, st, s, st, st),
-        in_specs=[ANY, ANY, pl.BlockSpec((1, D, C), lambda j: (0, 0, j)), pl.BlockSpec((1, D, C), lambda j: (0, 0, j)), ANY],
+        in_specs=[ANY, ANY, pl.BlockSpec((1, D, CF), lambda j: (0, 0, j)), pl.BlockSpec((1, D, CF), lambda j: (0, 0, j)), ANY],
         out_specs=[ANY] * 6,
         scratch_shapes=[v, v, v, vt, vt, pltpu.VMEM((T, FF), BF), pltpu.VMEM((FF, D), BF), v, v, vt, pltpu.SemaphoreType.DMA((32,))],
         compiler_params=cparams(dimension_semantics=("arbitrary",)),
@@ -88,9 +91,9 @@
 V = 2 * U
 SUB = HALF // 2
 NR2 = 18
-STAGE2 = (2, 3, 3, 4, 5, 5, 6, 7, 7, 8, 9, 9, 9, 10, 11, 12, 13, 14, 14, 15, 16, 17)
-STAGE3 = (4, 4, 5, 6, 6, 7, 8, 8, 9, 10, 10, 10, 11, 12, 13, 14, 15, 15, 16, 17)
-STAGE4 = (5, 6, 7, 7, 8, 9, 9, 10, 11, 11, 11, 12, 13, 14, 15, 16, 16, 17)
+STAGE2 = (1, 2, 2, 3, 4, 4, 5, 5, 6, 6, 7, 8, 8, 9, 9, 9, 10, 11, 12, 12, 13, 14, 15, 15, 16, 17, 17)
+STAGE3 = (3, 3, 4, 5, 5, 6, 6, 7, 7, 8, 9, 9, 10, 10, 10, 11, 12, 13, 13, 14, 15, 16, 16, 17)
+STAGE4 = (4, 5, 6, 6, 7, 7, 8, 8, 9, 10, 10, 11, 11, 11, 12, 13, 14, 14, 15, 16, 17, 17)
 MESH = pl.DeviceIdType.MESH
 
 def upto(table, s):

time: 456 us -> 462 us (1.013)
  Pallas kernels: 455 us -> 461 us
    pallas_call x1, Pallas kernels: 328 us -> 334 us  [mega(): pl.pallas_call(mega_body, grid=(U,), name='backward', out_shape=jax.Shape...]
where the time goes in v3:
time: 462 us
  Pallas kernels  461 us (100%)
    pallas_call x1, Pallas kernels, mega(): pl.pallas_call(mega_body, grid=(U,), name='backward', out_shape=jax.Shape...  334 us
    pallas_call x1, Pallas kernels, adam(): pl.pallas_call(adam_body, grid=(U,), name='adam', in_specs=[pl.BlockSpec(...  88.6 us
    pallas_call x1, Pallas kernels, fwd(): pl.pallas_call(fwd_body, grid=(NF,), name='fwd0', out_shape=(s, s, st, s,...  38.4 us

profile of v3, /device:TPU:0, one launch (start us, length us, event | category | flops | bytes accessed | tf_op | source)
XLA Modules:
  0.0 462.2 jit_solution(13495897255760622590)
XLA Ops:
  0.6 38.4 %fwd0.1 = (bf16[2048,896]{1,0:T(8,128)(2,1)}, bf16[2048,896]{1,0:T(8,128)(2,1)}, bf16[896,2048]{1,0:T(8,128)(2,1)}, bf16[2048,896]{1,0:T(8,128)(2,1)}, bf16[896,...) custom-call(bf16[2048,896]{1,0:T(8,128)(2,1)} %bitcast.4, bf16[2048,896]{1,0:T(8,128)(2,1)} %bitcast.2, ...), custom_call_target="tpu_custom_call" | custom-call | tf_op jit(solution)/shard_map/fwd0/pallas_call | solution.py:81
  39.1 334.4 %backward.1.f_ref = bf16[18,2,1344,256]{3,2,1,0:T(8,128)(2,1)} custom-call(bf16[2048,896]{1,0:T(8,128)(2,1)} %get-tuple-element.15.a1_hbm, bf16[896,2048]{1,0:T(8,128)(2,1)} %get-tuple-element.16.a1t_hbm, bf16[2048,896]{1,0:T(8,128)(2,1)} %bitcast.3, bf16[896,2048]{1,0:T(8,128)(2,1)} %get-tuple-element.17.dyt_hbm, ...), custom_call_target="tpu_custom_call" | custom-call | tf_op jit(solution)/shard_map/backward/pallas_call | solution.py:285
  373.5 88.6 %adam.1 = (bf16[2,896,2304]{2,1,0:T(8,128)(2,1)}, bf16[2,896,2304]{2,1,0:T(8,128)(2,1)}, bf16[2,2304,896]{2,1,0:T(8,128)(2,1)}, f32[2,896,2304]{2,1,0:T(8,128)},...) custom-call(bf16[18,2,1344,256]{3,2,1,0:T(8,128)(2,1)} %backward.1.f, ...), custom_call_target="tpu_custom_call" | custom-call | tf_op jit(solution)/shard_map/adam/pallas_call | solution.py:311

commit v4 on v3

--- a/solution.py
+++ b/solution.py
@@ -91,9 +91,8 @@
 V = 2 * U
 SUB = HALF // 2
 NR2 = 18
-STAGE2 = (1, 2, 2, 3, 4, 4, 5, 5, 6, 6, 7, 8, 8, 9, 9, 9, 10, 11, 12, 12, 13, 14, 15, 15, 16, 17, 17)
-STAGE3 = (3, 3, 4, 5, 5, 6, 6, 7, 7, 8, 9, 9, 10, 10, 10, 11, 12, 13, 13, 14, 15, 16, 16, 17)
-STAGE4 = (4, 5, 6, 6, 7, 7, 8, 8, 9, 10, 10, 11, 11, 11, 12, 13, 14, 14, 15, 16, 17, 17)
+STAGE2 = (4, 5, 6, 8, 9, 10, 12, 13, 14, 16, 17, 18, 18, 20, 22, 24, 26, 27, 28, 30, 32, 34)
+STAGE3 = (6, 7, 9, 10, 11, 13, 14, 15, 17, 18, 19, 19, 21, 23, 25, 27, 28, 29, 31, 33, 35)
 MESH = pl.DeviceIdType.MESH
 
 def upto(table, s):
@@ -229,11 +228,8 @@
     def _(): stage1(s - 1)
     @pl.when(inner)
     def _():
-        lax.fori_loop(upto(STAGE2, s - 1), upto(STAGE2, s), stage2, 0)
-        lax.fori_loop(upto(STAGE3, s - 1), upto(STAGE3, s), stage3, 0)
-    @pl.when(outer)
-    def _():
-        lax.fori_loop(upto(STAGE4, s - 1), upto(STAGE4, s), stage4, 0)
+        lax.fori_loop(upto(STAGE2, 2 * s - 1), upto(STAGE2, 2 * s), stage2, 0)
+        lax.fori_loop(upto(STAGE3, 2 * s - 1), upto(STAGE3, 2 * s), stage3, 0)
 
     slot = lax.rem(s, 2)
     for tile in range(6):
@@ -250,6 +246,11 @@
             return c
         lax.fori_loop(0, T // RT, part, 0)
         stage1(s)
+
+    @pl.when(inner)
+    def _():
+        lax.fori_loop(upto(STAGE2, 2 * s), upto(STAGE2, 2 * s + 1), stage2, 0)
+        lax.fori_loop(upto(STAGE3, 2 * s), upto(STAGE3, 2 * s + 1), stage3, 0)
 
     @pl.when(s == U - 1)
     def _():
@@ -270,7 +271,7 @@
             lax.fori_loop(0, V, done, 0)
         @pl.when(outer)
         def _():
-            lax.fori_loop(len(STAGE4), V, stage4, 0)
+            lax.fori_loop(0, V, stage4, 0)
             def done(u, c):
                 cs1(u).wait_send()
                 cp4o(u).wait_send(); cp4o(u).wait_recv()

time: 462 us -> 449 us (0.972)
  Pallas kernels: 461 us -> 448 us
    pallas_call x1, Pallas kernels: 334 us -> 321 us  [mega(): pl.pallas_call(mega_body, grid=(U,), name='backward', out_shape=jax.Shape...]
where the time goes in v4:
time: 449 us
  Pallas kernels  448 us (100%)
    pallas_call x1, Pallas kernels, mega(): pl.pallas_call(mega_body, grid=(U,), name='backward', out_shape=jax.Shape...  321 us
    pallas_call x1, Pallas kernels, adam(): pl.pallas_call(adam_body, grid=(U,), name='adam', in_specs=[pl.BlockSpec(...  88.6 us
    pallas_call x1, Pallas kernels, fwd(): pl.pallas_call(fwd_body, grid=(NF,), name='fwd0', out_shape=(s, s, st, s,...  38.4 us

profile of v4, /device:TPU:0, one launch (start us, length us, event | category | flops | bytes accessed | tf_op | source)
XLA Modules:
  0.0 449.1 jit_solution(9549539726612161617)
XLA Ops:
  0.6 38.4 %fwd0.1 = (bf16[2048,896]{1,0:T(8,128)(2,1)}, bf16[2048,896]{1,0:T(8,128)(2,1)}, bf16[896,2048]{1,0:T(8,128)(2,1)}, bf16[2048,896]{1,0:T(8,128)(2,1)}, bf16[896,...) custom-call(bf16[2048,896]{1,0:T(8,128)(2,1)} %bitcast.4, bf16[2048,896]{1,0:T(8,128)(2,1)} %bitcast.2, ...), custom_call_target="tpu_custom_call" | custom-call | tf_op jit(solution)/shard_map/fwd0/pallas_call | solution.py:81
  39.1 321.3 %backward.1.f_ref = bf16[18,2,1344,256]{3,2,1,0:T(8,128)(2,1)} custom-call(bf16[2048,896]{1,0:T(8,128)(2,1)} %get-tuple-element.15.a1_hbm, bf16[896,2048]{1,0:T(8,128)(2,1)} %get-tuple-element.16.a1t_hbm, bf16[2048,896]{1,0:T(8,128)(2,1)} %bitcast.3, bf16[896,2048]{1,0:T(8,128)(2,1)} %get-tuple-element.17.dyt_hbm, ...), custom_call_target="tpu_custom_call" | custom-call | tf_op jit(solution)/shard_map/backward/pallas_call | solution.py:286
  360.4 88.6 %adam.1 = (bf16[2,896,2304]{2,1,0:T(8,128)(2,1)}, bf16[2,896,2304]{2,1,0:T(8,128)(2,1)}, bf16[2,2304,896]{2,1,0:T(8,128)(2,1)}, f32[2,896,2304]{2,1,0:T(8,128)},...) custom-call(bf16[18,2,1344,256]{3,2,1,0:T(8,128)(2,1)} %backward.1.f, ...), custom_call_target="tpu_custom_call" | custom-call | tf_op jit(solution)/shard_map/adam/pallas_call | solution.py:312
